TPU v7x, 32 devices: a whole 2x2x4 slice. The times are simulated.
32 devices in a mesh: groups: 2 (over y), seq: 4 (over z), head: 4 (over x, core).
Axes of the slice: x: 2, y: 2, z: 4, core: 2. Of those that a mesh axis runs over, the one named last changes fastest.
Arguments:
- queries: bfloat16 [32, 3, 32, 128], P('groups', None, 'head'), parts along dimension 0, may hold values from -8 to 8
- new_kv: bfloat16 [4, 16, 3, 4, 128], P('groups', None, None, 'head'), parts along dimension 0, may hold values from -16 to 16
- res_kv: bfloat16 [4, 2, 16384, 4, 128], P('groups', None, 'seq', 'head'), parts along dimension 0, may hold values from -16 to 16
- prefill_kv: bfloat16 [4, 4, 4096, 128], P('groups', None, ('seq', 'head')), parts along dimension 0, may hold values from -16 to 16
- block_table: int32 [128], P('groups'), parts along dimension 0, may hold values from 0 to 63, as said below
- lengths: int32 [6], P('groups'), parts along dimension 0, may hold values from 4096 to 16384, as said below
- join_step: int32 [2], P('groups'), parts along dimension 0, may hold values from 1 to 15
Outputs:
- attn_out: bfloat16 [32, 3, 32, 128], P('groups', None, 'head'), parts along dimension 0
- new_cache: bfloat16 [4, 4, 4096, 128], P('groups', 'head', 'seq'), parts along dimension 0
There are 2 independent parts, one for each index of `groups`. A program takes and returns all parts, laid end to end along the dimension named above; each array names one. Nothing has to cross between parts.
Inputs may be any that keep to these rules, and one draw needn't show every extreme that they name: `block_table`: A permutation of 0 to 63. In each aligned run of 4 entries (the blocks of one prefill device) every aligned range of 16 slots is named exactly 1 times. `lengths`: entries 0 to 1 lie between 4096 and 16384, and one of them equals 16384; entry 2 equals 4096.
All inputs are finite; a program needn't handle non-finite values.
Results may differ from a plain program's by a relative error of at most 0.0039.
Values may be sent and summed in bfloat16 or wider, within the bound.
A program may use at most 64 MiB of HBM per device.

v0:
```python
import functools
import math

import jax
import jax.numpy as jnp
from jax import lax
from jax.experimental import pallas as pl
from jax.experimental.pallas import tpu as pltpu
from jax.sharding import PartitionSpec as P

very_low = -1e30
MESH = pl.DeviceIdType.MESH
NT = (((1,), (1,)), ((), ()))
TN = (((0,), (0,)), ((), ()))


def kernel(
    seq_count,
    head_count,
    queries,
    fresh,
    prefill_kv,
    table,
    lengths,
    join_step,
    res_kv,
    attn_out,
    new_cache,
    prefill,
    res_buf,
    staged,
    arrived,
    own_acc,
    own_stat,
    fresh_acc,
    fresh_stat,
    out_acc,
    out_stat,
    got_acc,
    got_stat,
    slice_send,
    slice_got,
    whole_out,
    slot_of,
    base_of,
    prefill_sem,
    res_sem,
    block_sems,
    acc_send,
    acc_recv,
    stat_send,
    stat_recv,
    slice_sems,
    whole_sems,
):
    seq_index = lax.axis_index("seq")
    head_index = lax.axis_index("head")
    senders = seq_count * head_count
    me = seq_index * head_count + head_index
    step_count, request_count, group_size, head_dim = queries.shape
    rows = step_count * group_size
    resident = res_kv.shape[1]
    res_rows = res_kv.shape[2]
    dev_blocks, block_len = prefill.shape[2], prefill.shape[3]
    slot_count = senders * dev_blocks // seq_count
    scale = 1.0 / math.sqrt(head_dim)
    joined = join_step[0]
    part_dim = head_dim // seq_count
    peers = [lax.rem(seq_index + o, seq_count) for o in range(1, seq_count)]

    fetch = pltpu.make_async_copy(prefill_kv, prefill, prefill_sem)
    fetch.start()
    barrier = pltpu.get_barrier_semaphore()

    def greet(o, _):
        peer = lax.rem(me + o, senders)
        pl.semaphore_signal(
            barrier,
            inc=1,
            device_id={"seq": peer // head_count, "head": lax.rem(peer, head_count)},
            device_id_type=MESH,
        )
        return 0

    lax.fori_loop(1, senders, greet, 0)

    res_copies = []
    for r in range(resident):
        for c in range(2):
            copy = pltpu.make_async_copy(res_kv.at[c, r], res_buf.at[c, r], res_sem.at[c, r])
            copy.start()
            res_copies.append(copy)

    def block_for(sender, shard):
        found = jnp.int32(0)
        slot = jnp.int32(0)
        for k in range(dev_blocks):
            here = table[sender * dev_blocks + k]
            hit = (here // slot_count) == shard
            found = jnp.where(hit, k, found)
            slot = jnp.where(hit, here, slot)
        return found, slot

    def stage(z, _):
        found, _slot = block_for(me, z)
        for h in range(head_count):
            for c in range(2):
                staged[z * head_count + h, c] = prefill[c, h, found]
        return 0

    fetch.wait()
    lax.fori_loop(0, seq_count, stage, 0)
    pl.semaphore_wait(barrier, senders - 1)

    def send(o, _):
        peer = lax.rem(me + o, senders)
        pltpu.make_async_remote_copy(
            src_ref=staged.at[peer],
            dst_ref=arrived.at[me],
            send_sem=block_sems.at[0],
            recv_sem=block_sems.at[1],
            device_id={"seq": peer // head_count, "head": lax.rem(peer, head_count)},
            device_id_type=MESH,
        ).start()
        return 0

    lax.fori_loop(1, senders, send, 0)
    arrived[me] = staged[me]

    def locate(s, _):
        found, slot = block_for(s, seq_index)
        slot_of[s] = slot - seq_index * slot_count
        base_of[s] = (s * dev_blocks + found) * block_len
        return 0

    lax.fori_loop(0, senders, locate, 0)

    def query_rows(r):
        wide = queries[:, r].astype(jnp.float32).reshape(rows, head_dim)
        return wide.astype(jnp.bfloat16)

    def fold(carry, keys, values, valid, q):
        m, l, acc = carry
        s = lax.dot_general(keys, q, NT, preferred_element_type=jnp.float32) * scale
        s = jnp.where(valid, s, very_low)
        top = jnp.maximum(m, jnp.max(s, axis=0, keepdims=True))
        w = jnp.where(valid, jnp.exp(s - top), 0.0)
        keep = jnp.exp(m - top)
        l = l * keep + jnp.sum(w, axis=0, keepdims=True)
        acc = acc * keep + lax.dot_general(
            values, w.astype(jnp.bfloat16), TN, preferred_element_type=jnp.float32
        )
        return top, l, acc

    empty = (
        jnp.full((1, rows), very_low, jnp.float32),
        jnp.zeros((1, rows), jnp.float32),
        jnp.zeros((head_dim, rows), jnp.float32),
    )

    chunk = math.gcd(res_rows, 1024)
    for r in range(resident):
        q = query_rows(r)
        res_copies[2 * r].wait()
        res_copies[2 * r + 1].wait()
        limit = lengths[r] - seq_index * res_rows

        def step(i, carry, r=r, q=q, limit=limit):
            at = pl.ds(pl.multiple_of(i * chunk, chunk), chunk)
            valid = lax.broadcasted_iota(jnp.int32, (chunk, rows), 0) + i * chunk < limit
            return fold(carry, res_buf[0, r, at], res_buf[1, r, at], valid, q)

        m, l, acc = lax.fori_loop(0, res_rows // chunk, step, empty)
        own_stat[2 * r : 2 * r + 1] = m
        own_stat[2 * r + 1 : 2 * r + 2] = l
        own_acc[r] = acc
        pieces = acc.reshape(seq_count, part_dim, rows).astype(jnp.bfloat16)
        for z in range(seq_count):
            slice_send[z, r] = pieces[z]
        out_stat[0, 2 * r : 2 * r + 1] = m
        out_stat[0, 2 * r + 1 : 2 * r + 2] = l

    when = lax.broadcasted_iota(jnp.int32, (step_count, rows), 1) // group_size
    which = lax.broadcasted_iota(jnp.int32, (step_count, rows), 0)
    for r in range(request_count):
        allowed = which <= when
        if r >= resident:
            allowed = allowed & (which >= joined)
        m, l, acc = fold(empty, fresh[0, r], fresh[1, r], allowed, query_rows(r))
        fresh_stat[2 * r : 2 * r + 1] = m
        fresh_stat[2 * r + 1 : 2 * r + 2] = l
        fresh_acc[r] = acc

    def remote(source, target, send_sem, recv_sem, peer):
        pltpu.make_async_remote_copy(
            src_ref=source,
            dst_ref=target,
            send_sem=send_sem,
            recv_sem=recv_sem,
            device_id={"seq": peer},
            device_id_type=MESH,
        ).start()

    def drain(buffer, sem):
        part = buffer.at[pl.ds(0, seq_count - 1)]
        pltpu.make_async_copy(part, part, sem).wait()

    def push_stat(phase):
        for peer in peers:
            remote(
                out_stat.at[phase],
                got_stat.at[phase, seq_index],
                stat_send.at[phase],
                stat_recv.at[phase],
                peer,
            )

    def merge(r, phase, row, own, new, got):
        maxima = [own_stat[2 * r : 2 * r + 1], fresh_stat[2 * r : 2 * r + 1]]
        totals = [own_stat[2 * r + 1 : 2 * r + 2], fresh_stat[2 * r + 1 : 2 * r + 2]]
        for peer in peers:
            maxima.append(got_stat[phase, peer, row : row + 1])
            totals.append(got_stat[phase, peer, row + 1 : row + 2])
        top = functools.reduce(jnp.maximum, maxima)
        factors = [jnp.exp(m - top) for m in maxima]
        total = sum(f * t for f, t in zip(factors, totals))
        summed = own * factors[0] + new * factors[1]
        for peer, f in zip(peers, factors[2:]):
            summed = summed + got(peer).astype(jnp.float32) * f
        return summed / total

    push_stat(0)
    for peer in peers:
        remote(slice_send.at[peer], slice_got.at[seq_index], slice_sems.at[0], slice_sems.at[1], peer)

    drain(got_stat.at[0], stat_recv.at[0])
    drain(slice_got, slice_sems.at[1])
    mine = pl.ds(pl.multiple_of(seq_index * part_dim, part_dim), part_dim)
    for r in range(resident):
        whole_out[seq_index, r] = merge(
            r, 0, 2 * r, own_acc[r, mine], fresh_acc[r, mine], lambda peer: slice_got[peer, r]
        ).astype(jnp.bfloat16)
    for peer in peers:
        remote(
            whole_out.at[seq_index], whole_out.at[seq_index], whole_sems.at[0], whole_sems.at[1], peer
        )

    part = arrived.at[pl.ds(0, senders - 1)]
    pltpu.make_async_copy(part, part, block_sems.at[1]).wait()

    q = query_rows(resident)
    some = math.gcd(senders, 16)

    def step(i, carry):
        first = i * some
        keys = arrived[pl.ds(first, some), 0].reshape(some * block_len, head_dim)
        values = arrived[pl.ds(first, some), 1].reshape(some * block_len, head_dim)
        offsets = lax.broadcasted_iota(jnp.int32, (block_len, rows), 0)
        positions = jnp.concatenate([offsets + base_of[first + s] for s in range(some)], axis=0)
        return fold(carry, keys, values, positions < lengths[resident], q)

    m, l, acc = lax.fori_loop(0, senders // some, step, empty)
    out_acc[...] = acc.astype(jnp.bfloat16)
    out_stat[1, 0:1] = m
    out_stat[1, 1:2] = l
    own_stat[2 * resident : 2 * resident + 1] = m
    own_stat[2 * resident + 1 : 2 * resident + 2] = l
    own_acc[resident] = acc
    push_stat(1)
    for peer in peers:
        remote(out_acc, got_acc.at[seq_index], acc_send, acc_recv, peer)

    def place(j, _):
        def look(s, found):
            return jnp.where(slot_of[s] == j, s, found)

        source = lax.fori_loop(0, senders, look, jnp.int32(0), unroll=math.gcd(senders, 16))
        at = pl.ds(pl.multiple_of(j * block_len, block_len), block_len)
        for c in range(2):
            new_cache[c, 0, at] = arrived[source, c]
        return 0

    lax.fori_loop(0, slot_count, place, 0)

    def finish(r, result):
        result = jnp.transpose(result).reshape(step_count, group_size, head_dim)
        attn_out[:, r] = result.astype(jnp.bfloat16)

    drain(whole_out, whole_sems.at[1])
    for r in range(resident):
        pieces = [whole_out[z, r].astype(jnp.float32) for z in range(seq_count)]
        finish(r, jnp.concatenate(pieces, axis=0))
    drain(got_stat.at[1], stat_recv.at[1])
    drain(got_acc, acc_recv)
    r = resident
    result = merge(r, 1, 0, own_acc[r], fresh_acc[r], lambda peer: got_acc[peer])
    lane = lax.broadcasted_iota(jnp.int32, (head_dim, rows), 1) // group_size
    finish(r, jnp.where(lane >= joined, result, 0.0))

    part = staged.at[pl.ds(0, senders - 1)]
    pltpu.make_async_copy(part, part, block_sems.at[0]).wait()
    drain(got_stat.at[0], stat_send.at[0])
    drain(slice_got, slice_sems.at[0])
    drain(whole_out, whole_sems.at[0])
    drain(got_stat.at[1], stat_send.at[1])
    drain(got_acc, acc_send)


def per_device(seq_count, head_count, queries, new_kv, res_kv, prefill_kv, block_table, lengths, join_step):
    step_count, request_count, group_size, head_dim = queries.shape
    rows = step_count * group_size
    resident, res_rows = res_kv.shape[1], res_kv.shape[2]
    head_total, new_rows = prefill_kv.shape[1], prefill_kv.shape[2]
    senders = seq_count * head_count
    dev_blocks = block_table.shape[0] // senders
    block_len = new_rows // dev_blocks
    if dev_blocks != seq_count or resident > 4 or head_total != head_count:
        raise ValueError("unsupported sizes")
    slot_count = block_table.shape[0] // seq_count
    fresh = jnp.transpose(new_kv[:, :, :, 0], (0, 2, 1, 3))
    prefill = prefill_kv.reshape(2, head_total, dev_blocks, block_len, head_dim)
    part_dim = head_dim // seq_count
    out_bytes = 2 * (queries.size + 2 * slot_count * block_len * head_dim)
    vmem = pl.BlockSpec(memory_space=pltpu.VMEM)
    smem = pl.BlockSpec(memory_space=pltpu.SMEM)
    hbm = pl.BlockSpec(memory_space=pltpu.HBM)
    bf16, f32 = jnp.bfloat16, jnp.float32
    return pl.pallas_call(
        functools.partial(kernel, seq_count, head_count),
        out_shape=(
            pltpu.VMEM(queries.shape, bf16),
            pltpu.VMEM((2, 1, slot_count * block_len, head_dim), bf16),
        ),
        in_specs=[vmem, vmem, hbm, smem, smem, smem, hbm],
        out_specs=(vmem, vmem),
        scratch_shapes=[
            pltpu.VMEM(prefill.shape, bf16),
            pltpu.VMEM((2, resident, res_rows, head_dim), bf16),
            pltpu.VMEM((senders, 2, block_len, head_dim), bf16),
            pltpu.VMEM((senders, 2, block_len, head_dim), bf16),
            pltpu.VMEM((request_count, head_dim, rows), f32),
            pltpu.VMEM((16, rows), f32),
            pltpu.VMEM((request_count, head_dim, rows), f32),
            pltpu.VMEM((16, rows), f32),
            pltpu.VMEM((head_dim, rows), bf16),
            pltpu.VMEM((2, 8, rows), f32),
            pltpu.VMEM((seq_count, head_dim, rows), bf16),
            pltpu.VMEM((2, seq_count, 8, rows), f32),
            pltpu.VMEM((seq_count, resident, part_dim, rows), bf16),
            pltpu.VMEM((seq_count, resident, part_dim, rows), bf16),
            pltpu.VMEM((seq_count, resident, part_dim, rows), bf16),
            pltpu.SMEM((senders,), jnp.int32),
            pltpu.SMEM((senders,), jnp.int32),
            pltpu.SemaphoreType.DMA,
            pltpu.SemaphoreType.DMA((2, resident)),
            pltpu.SemaphoreType.DMA((2,)),
            pltpu.SemaphoreType.DMA,
            pltpu.SemaphoreType.DMA,
            pltpu.SemaphoreType.DMA((2,)),
            pltpu.SemaphoreType.DMA((2,)),
            pltpu.SemaphoreType.DMA((2,)),
            pltpu.SemaphoreType.DMA((2,)),
        ],
        compiler_params=pltpu.CompilerParams(
            collective_id=0, has_side_effects=True, vmem_limit_bytes=62 * 2**20 - 3 * out_bytes
        ),
    )(
        queries,
        fresh,
        prefill,
        block_table,
        lengths,
        join_step,
        res_kv.reshape(2, resident, res_rows, head_dim),
    )


def solution(mesh):
    in_specs = (
        P("groups", None, "head", None),
        P("groups", None, None, "head", None),
        P("groups", None, "seq", "head", None),
        P("groups", None, ("seq", "head"), None),
        P("groups"),
        P("groups"),
        P("groups"),
    )
    out_specs = (P("groups", None, "head", None), P("groups", "head", "seq", None))
    body = functools.partial(per_device, mesh.shape["seq"], mesh.shape["head"])
    return jax.shard_map(body, mesh=mesh, in_specs=in_specs, out_specs=out_specs, check_vma=False)
```

profile of v0, /device:TPU:0, one launch (start us, length us, event | category | flops | bytes accessed | tf_op | source)
XLA Modules:
  0.0 30.4 jit_solution(18360496006515488229)
XLA Ops:
  1.3 27.7 %shard_map.86 = (bf16[16,3,8,128]{3,2,1,0:T(8,128)(2,1)S(1)}, bf16[2,1,1024,128]{3,2,1,0:T(8,128)(2,1)S(1)}) custom-call(bf16[16,3,8,128]{3,2,1,0:T(8,128)(2,1)} %queries.1, bf16[2,3,16,128]{3,2,1,0:T(8,128)(2,1)} %bitcast.7, bf16[2,4,4,64,128]{4,3,2,1,0:T(8,128)(2,1)} %bitcast.6, s32[64]{0:T(128)} %table.1, s32[3]{0:T(128)} %lengths.1, ...), custom_call_target="tpu_custom_call" | custom-call | tf_op jit(solution)/shard_map/pallas_call | solution.py:328
  28.9 0.6 %copy.11 = bf16[16,3,8,128]{3,2,1,0:T(8,128)(2,1)} copy(bf16[16,3,8,128]{3,2,1,0:T(8,128)(2,1)S(1)} %get-tuple-element.2) | data formatting | bytes 196608
  29.6 0.8 %copy.12 = bf16[2,1,1024,128]{3,2,1,0:T(8,128)(2,1)} copy(bf16[2,1,1024,128]{3,2,1,0:T(8,128)(2,1)S(1)} %get-tuple-element.3) | data formatting | bytes 1048576
where the time goes:
time: 30.5 us; the launch traced here: 30.4 us
  Pallas kernels  27.7 us (91%)
  local copies, waits for them, and re-layouts  1.44 us (5%)
  between operations  1.29 us (4%)
    pallas_call x1, Pallas kernels, per_device(): pl.pallas_call(functools.partial(kernel, seq_count, head_count), out_shap...  27.7 us
    unnamed x2, local copies, waits for them, and re-layouts  1.44 us

commit v1 on v0

v1 whole, which is shorter than its diff:
```python
import functools
import math
import types

import jax
import jax.numpy as jnp
from jax import lax
from jax.experimental import pallas as pl
from jax.experimental.pallas import tpu as pltpu
from jax.sharding import PartitionSpec as P

very_low = -1e30
MESH = pl.DeviceIdType.MESH
NT = (((1,), (1,)), ((), ()))
NN = (((1,), (0,)), ((), ()))


def split_of(count):
    inner = 1
    for d in range(1, count + 1):
        if count % d == 0 and d * d <= count:
            inner = d
    return inner, count // inner


def named(groups):
    space = types.SimpleNamespace()
    for group in groups:
        for name, value in group.items():
            setattr(space, name, named([value]) if isinstance(value, dict) else value)
    return space


def kernel(seq_count, head_count, tree, *leaves):
    ref = named(jax.tree.unflatten(tree, leaves))
    q_hbm, fresh_hbm, prefill_hbm, res_hbm = ref.q_hbm, ref.fresh_hbm, ref.prefill_hbm, ref.res_hbm
    attn_out, cache_out = ref.attn_out, ref.cache_out
    table, lengths, joins = ref.table, ref.lengths, ref.joins
    arrived = ref.arrived
    inner, outer = split_of(seq_count)
    seq_index = lax.axis_index("seq")
    head_index = lax.axis_index("head")
    group = seq_index // inner

    def fold_back(g, p):
        return jnp.where(lax.rem(g, 2) == 0, p, inner - 1 - p)

    def member(g, p):
        return g * inner + fold_back(g, p)

    place_in = fold_back(group, lax.rem(seq_index, inner))
    step_count, request_count, group_size, head_dim = q_hbm.shape
    rows = step_count * group_size
    resident, res_rows = res_hbm.shape[1], res_hbm.shape[2]
    dev_blocks, block_len = prefill_hbm.shape[2], prefill_hbm.shape[3]
    senders = seq_count * head_count
    slot_count = senders * dev_blocks // seq_count
    per_dev = dev_blocks * block_len
    part, step_part = rows // inner, step_count // inner
    power = math.log2(math.e) / math.sqrt(head_dim)
    heads = [head_index] + [head_index ^ o for o in range(1, head_count)]
    held = ref.held
    staged = ref.staged

    barrier = pltpu.get_barrier_semaphore()

    def greet(**device):
        pl.semaphore_signal(barrier, inc=1, device_id=device, device_id_type=MESH)

    above, below = seq_index + 1 < seq_count, seq_index > 0
    pl.when(above)(lambda: greet(seq=seq_index + 1))
    pl.when(below)(lambda: greet(seq=seq_index - 1))
    for o in range(1, head_count):
        greet(head=heads[o])

    def tell(d):
        if d + 1 < seq_count:
            for sem, there, on, step in ((ref.above_sems, 1, below, -1), (ref.below_sems, -1, above, 1)):
                far = seq_index + there * d

                @pl.when((far >= 0) & (far < seq_count) & on)
                def _(sem=sem, step=step):
                    pl.semaphore_signal(
                        sem.at[d - 1], inc=1, device_id={"seq": seq_index + step}, device_id_type=MESH
                    )

    def learn(d):
        pl.when(seq_index + d < seq_count)(lambda: pl.semaphore_wait(ref.above_sems.at[d - 2], 1))
        pl.when(seq_index - d >= 0)(lambda: pl.semaphore_wait(ref.below_sems.at[d - 2], 1))
        tell(d)

    def local(source, target, sem):
        copy = pltpu.make_async_copy(source, target, sem)
        copy.start()
        return copy

    table_copy = local(ref.table_hbm, table, ref.table_sem)
    own_copy = local(prefill_hbm.at[:, head_index], held[0], ref.own_sem)
    q_copy = local(q_hbm, ref.q_buf, ref.q_sem)
    fresh_copy = local(fresh_hbm, ref.fresh_buf, ref.fresh_sem)
    length_copy = local(ref.lengths_hbm, lengths, ref.lengths_sem)
    join_copy = local(ref.joins_hbm, joins, ref.joins_sem)
    table_copy.wait()
    own_copy.wait()
    chunk = math.gcd(res_rows, 2048)
    chunks = res_rows // chunk
    res_copies = []
    for r in range(resident):
        for k in range(chunks):
            at = pl.ds(k * chunk, chunk)
            res_copies.append(local(res_hbm.at[:, r, at], ref.res_buf.at[:, r, at], ref.res_sems.at[r, k]))

    def remote(source, target, send_sem, recv_sem, **device):
        pltpu.make_async_remote_copy(
            src_ref=source, dst_ref=target, send_sem=send_sem, recv_sem=recv_sem, device_id=device, device_id_type=MESH
        ).start()

    def drain(part_ref, sem):
        pltpu.make_async_copy(part_ref, part_ref, sem).wait()

    def block_for(sender, shard):
        found = jnp.int32(0)
        for k in range(dev_blocks):
            hit = (table[sender * dev_blocks + k] // slot_count) == shard
            found = jnp.where(hit, k, found)
        return found

    def stage(o):
        sender = seq_index * head_count + heads[o]

        def body(z, _):
            found = block_for(sender, z)
            for c in range(2):
                staged[o][z, c] = held[o][c, found]
            return 0

        lax.fori_loop(0, seq_count, body, 0, unroll=seq_count <= 4)
        arrived[seq_index, heads[o]] = staged[o][seq_index]

    def forward(o, distances, inside=None, only=None):
        for d in distances:
            for peer in (seq_index - d, seq_index + d):

                wanted = (peer >= 0) & (peer < seq_count)
                if inside is not None:
                    wanted = wanted & ((peer // inner == group) == inside)

                if only is not None:
                    wanted = wanted & only

                @pl.when(wanted)
                def _(peer=peer):
                    target = arrived.at[seq_index, heads[o]]
                    remote(staged[o].at[peer], target, ref.block_send, ref.block_recv, seq=peer)

    def hand(o):
        remote(prefill_hbm.at[:, heads[o]], held[o], ref.held_send, ref.held_recv.at[o], head=heads[o])

    far_first = range(seq_count - 1, 0, -1)
    stage(0)
    pl.semaphore_wait(barrier, head_count - 1 + above.astype(jnp.int32) + below.astype(jnp.int32))
    tell(1)
    for o in range(1, min(3, head_count)):
        hand(o)
    forward(0, [1])

    def query_rows(r):
        wide = ref.q_buf[:, r].astype(jnp.float32).reshape(rows, head_dim)
        return wide.astype(jnp.bfloat16)

    def fold(carry, q, keys, values, valid):
        s = lax.dot_general(q, keys, NT, preferred_element_type=jnp.float32)
        s = jnp.where(valid, s, very_low)
        top = jnp.max(s, axis=1, keepdims=True)
        if carry is not None:
            top = jnp.maximum(carry[0], top)
        w = jnp.exp2((s - top) * power)
        l = jnp.sum(w, axis=1, keepdims=True)
        acc = lax.dot_general(w.astype(jnp.bfloat16), values, NN, preferred_element_type=jnp.float32)
        if carry is not None:
            keep = jnp.exp2((carry[0] - top) * power)
            l = carry[1] * keep + l
            acc = carry[2] * keep + acc
        return top, l, acc

    length_copy.wait()
    join_copy.wait()
    joined = joins[0, 0]
    q_copy.wait()
    fresh_copy.wait()

    when = lax.broadcasted_iota(jnp.int32, (rows, step_count), 0) // group_size
    which = lax.broadcasted_iota(jnp.int32, (rows, step_count), 1)

    def fold_fresh(carry, r, q):
        allowed = (which <= when) & (seq_index == seq_count - 1)
        if r >= resident:
            allowed = allowed & (which >= joined)
        return fold(carry, q, ref.fresh_buf[0, r], ref.fresh_buf[1, r], allowed)

    def attend_resident(r, between=lambda k: None):
        q = query_rows(r)
        limit = lengths[r] - seq_index * res_rows
        carry = None
        for k in range(chunks):
            res_copies[r * chunks + k].wait()
            at = pl.ds(k * chunk, chunk)
            valid = lax.broadcasted_iota(jnp.int32, (1, chunk), 1) < limit - k * chunk
            carry = fold(carry, q, ref.res_buf[0, r, at], ref.res_buf[1, r, at], valid)
            between(k)
        return fold_fresh(carry, r, q)

    lane = lax.broadcasted_iota(jnp.int32, (rows, rows), 1)

    class Batch:
        def __init__(self, refs, first, results, split):
            self.refs, self.first, self.count, self.split = refs, first, len(results), split and inner > 1
            self.size = part if self.split else rows
            self.mine = pl.ds(pl.multiple_of(place_in * part, part), part) if self.split else slice(0, rows)
            for k, (m, l, acc) in enumerate(results):
                refs.acc[k] = acc
                refs.sent[k] = acc.astype(jnp.bfloat16)
            self.pack(refs.stat, [r[:2] for r in results])
            for oi in range(1, inner):
                to_inner = lax.rem(place_in + oi, inner)
                peer, back = member(group, to_inner), inner - oi
                self.share(refs.stat, back, refs.stat_sems, peer)
                source = refs.sent
                if self.split:
                    source = source.at[:, pl.ds(pl.multiple_of(to_inner * part, part), part)]
                remote(source, refs.got.at[back], refs.got_sems.at[0], refs.got_sems.at[1], seq=peer)

        def pack(self, target, stats):
            count = stats[0][0].shape[0]
            packed = jnp.zeros((count, rows), jnp.float32)
            for k, (m, l) in enumerate(stats):
                packed = jnp.where(lane[0:count] == 2 * k, m, packed)
                packed = jnp.where(lane[0:count] == 2 * k + 1, l, packed)
            if count < rows:
                packed = jnp.concatenate([packed, jnp.zeros((rows - count, rows), jnp.float32)], axis=0)
            tile = jnp.transpose(packed)[0:8]
            target[0:8] = tile
            self.refs.stat_send[0 if target is self.refs.stat else 1] = tile

        def share(self, target, back, sems, peer):
            source = self.refs.stat_send.at[0 if target is self.refs.stat else 1]
            remote(source, target.at[pl.ds(8 * back, 8)], sems.at[0], sems.at[1], seq=peer)

        def columns(self, tiles, members):
            stats = tiles[0 : 8 * members]
            if 8 * members < rows:
                stats = jnp.concatenate([stats, jnp.zeros((rows - 8 * members, rows), jnp.float32)], axis=0)
            return jnp.transpose(stats)

        def combine(self, turned, members, k):
            maxima = [turned[:, 8 * z + 2 * k : 8 * z + 2 * k + 1] for z in members]
            totals = [turned[:, 8 * z + 2 * k + 1 : 8 * z + 2 * k + 2] for z in members]
            top = functools.reduce(jnp.maximum, maxima)
            factors = [jnp.exp2((m - top) * power) for m in maxima]
            return top, sum(f * t for f, t in zip(factors, totals)), factors

        def across(self):
            refs = self.refs
            if inner > 1:
                drain(refs.stat.at[pl.ds(8, 8 * (inner - 1))], refs.stat_sems.at[1])
            turned = self.columns(refs.stat, inner)
            if self.split:
                ref.turned[...] = turned
                turned = ref.turned[self.mine]
            if inner > 1:
                drain(refs.got.at[pl.ds(1, inner - 1)], refs.got_sems.at[1])
            stats = []
            for k in range(self.count):
                top, total, factors = self.combine(turned, range(inner), k)
                summed = refs.acc[k, self.mine] * factors[0]
                for oi in range(1, inner):
                    summed = summed + refs.got[oi, k].astype(jnp.float32) * factors[oi]
                refs.level[0, k] = (summed / total).astype(jnp.bfloat16)
                stats.append((top, total))
            self.pack(refs.group_stat, stats)
            for og in range(1, outer):
                peer = member(lax.rem(group + og, outer), place_in)
                self.share(refs.group_stat, outer - og, refs.group_sems, peer)
                target = refs.level.at[outer - og]
                remote(refs.level.at[0], target, refs.level_sems.at[0], refs.level_sems.at[1], seq=peer)

        def finish(self):
            refs, level = self.refs, self.refs.level
            drain(refs.group_stat.at[pl.ds(8, 8 * (outer - 1))], refs.group_sems.at[1])
            turned = self.columns(refs.group_stat, outer)[0 : self.size]
            drain(level.at[pl.ds(1, outer - 1)], refs.level_sems.at[1])
            offset = place_in * step_part if self.split else 0
            steps = pl.ds(offset, self.size // group_size)
            for k in range(self.count):
                _, whole, factors = self.combine(turned, range(outer), k)
                result = jnp.zeros((self.size, head_dim), jnp.float32)
                for g in range(outer):
                    total = turned[:, 8 * g + 2 * k + 1 : 8 * g + 2 * k + 2]
                    result = result + level[g, k].astype(jnp.float32) * (factors[g] * total / whole)
                if self.first + k >= resident:
                    at = lax.broadcasted_iota(jnp.int32, (self.size, head_dim), 0) // group_size
                    result = jnp.where(at + offset >= joined, result, 0.0)
                result = result.reshape(self.size // group_size, group_size, head_dim)
                attn_out[steps, self.first + k] = result.astype(jnp.bfloat16)
            if self.split:
                piece = attn_out.at[steps, pl.ds(self.first, self.count)]
                for oi in range(1, inner):
                    peer = member(group, lax.rem(place_in + oi, inner))
                    remote(piece, piece, refs.final_sems.at[0], refs.final_sems.at[1], seq=peer)

        def close(self):
            refs = self.refs
            if self.split:
                others = attn_out.at[pl.ds(0, step_part * (inner - 1)), pl.ds(self.first, self.count)]
                drain(others, refs.final_sems.at[1])
                drain(others, refs.final_sems.at[0])
            if inner > 1:
                drain(refs.got.at[pl.ds(1, inner - 1)], refs.got_sems.at[0])
                drain(refs.stat.at[pl.ds(8, 8 * (inner - 1))], refs.stat_sems.at[0])
            drain(refs.group_stat.at[pl.ds(8, 8 * (outer - 1))], refs.group_sems.at[0])
            drain(refs.level.at[pl.ds(1, outer - 1)], refs.level_sems.at[0])

    def take(o):
        drain(held[o], ref.held_recv.at[o])
        stage(o)

    def between(k):
        if k == 0 and seq_count > 2:
            learn(2)
            forward(0, [2])

    results = [attend_resident(0, between)]
    for o in range(3, head_count):
        hand(o)
    for d in range(3, seq_count):
        learn(d)
        forward(0, [d])
    take(1)
    forward(1, far_first, False)
    results += [attend_resident(r) for r in range(1, resident)]
    batch_a = Batch(ref.batch_a, 0, results, True)
    forward(1, far_first, True)
    edge = (seq_index == 0) | (seq_index == seq_count - 1)

    q = query_rows(resident)

    def attend_new(carry, o):
        keys = held[o][0].reshape(per_dev, head_dim)
        values = held[o][1].reshape(per_dev, head_dim)
        base = (seq_index * head_count + heads[o]) * per_dev
        valid = lax.broadcasted_iota(jnp.int32, (1, per_dev), 1) + base < lengths[resident]
        return fold(carry, q, keys, values, valid)

    carry = fold_fresh(None, resident, q)
    for o in range(2):
        carry = attend_new(carry, o)
    for o in range(2, head_count - 1):
        take(o)
        forward(o, far_first, False, edge)
        carry = attend_new(carry, o)
    sources = ref.sources

    def locate(s, _):
        slot = jnp.int32(0)
        for k in range(dev_blocks):
            here = table[s * dev_blocks + k]
            slot = jnp.where((here // slot_count) == seq_index, here, slot)
        ref.slot_of[s] = slot - seq_index * slot_count
        return 0

    lax.fori_loop(0, senders, locate, 0)

    def source_for(j, _):
        def look(s, found):
            return jnp.where(ref.slot_of[s] == j, s, found)

        sources[j] = lax.fori_loop(0, senders, look, jnp.int32(0), unroll=math.gcd(senders, 16))
        return 0

    lax.fori_loop(0, slot_count, source_for, 0)

    batch_a.across()
    last = range(max(head_count - 1, 2), head_count)
    for o in range(2, head_count - 1):
        forward(o, far_first, False, jnp.logical_not(edge))
    for o in last:
        take(o)
        carry = attend_new(carry, o)
    batch_b = Batch(ref.batch_b, resident, [carry], False)
    for o in last:
        forward(o, far_first, False)
    for o in range(2, head_count - 1):
        forward(o, far_first, True)
    batch_b.across()
    for o in last:
        forward(o, far_first, True)
    batch_a.finish()
    batch_b.finish()

    part_ref = arrived.at[pl.ds(0, seq_count - 1)]
    drain(part_ref, ref.block_recv)

    def place(j, _):
        source = sources[j]
        at = pl.ds(pl.multiple_of(j * block_len, block_len), block_len)
        for c in range(2):
            cache_out[c, 0, at] = arrived[source // head_count, lax.rem(source, head_count), c]
        return 0

    lax.fori_loop(0, slot_count, place, 0, unroll=math.gcd(slot_count, 4))
    batch_a.close()
    batch_b.close()
    drain(part_ref, ref.block_send)
    for o in range(1, head_count):
        drain(held[o], ref.held_send)


def store_kernel(attn, cache, attn_out, cache_out, sems):
    copies = [pltpu.make_async_copy(cache.at[c], cache_out.at[c], sems.at[c]) for c in range(2)]
    copies.append(pltpu.make_async_copy(attn, attn_out, sems.at[2]))
    for copy in copies:
        copy.start()
    for copy in copies:
        copy.wait()


def per_device(seq_count, head_count, queries, new_kv, res_kv, prefill_kv, block_table, lengths, join_step):
    step_count, request_count, group_size, head_dim = queries.shape
    rows = step_count * group_size
    resident, res_rows = res_kv.shape[1], res_kv.shape[2]
    head_total, new_rows = prefill_kv.shape[1], prefill_kv.shape[2]
    senders = seq_count * head_count
    dev_blocks = block_table.shape[0] // senders
    block_len = new_rows // dev_blocks
    if dev_blocks != seq_count or resident > 3 or head_total != head_count:
        raise ValueError("unsupported sizes")
    if head_count & (head_count - 1) or head_count < 2 or seq_count < 2 or 8 * seq_count > rows or rows != head_dim:
        raise ValueError("unsupported sizes")
    inner, outer = split_of(seq_count)
    part = rows // inner
    slot_count = block_table.shape[0] // seq_count
    fresh = jnp.transpose(new_kv[:, :, :, 0], (0, 2, 1, 3))
    prefill = prefill_kv.reshape(2, head_total, dev_blocks, block_len, head_dim)
    bf16, f32, i32 = jnp.bfloat16, jnp.float32, jnp.int32
    vmem = pl.BlockSpec(memory_space=pltpu.VMEM)
    hbm = pl.BlockSpec(memory_space=pltpu.HBM)
    chunks = res_rows // math.gcd(res_rows, 2048)
    dma = pltpu.SemaphoreType.DMA
    def vm(dtype, *shape):
        return pltpu.VMEM(shape, dtype)

    def batch(count, size):
        return dict(
            acc=vm(f32, count, rows, head_dim),
            sent=vm(bf16, count, rows, head_dim),
            got=vm(bf16, inner, count, size, head_dim),
            level=vm(bf16, outer, count, size, head_dim),
            stat_send=vm(f32, 2, 8, rows),
            stat=vm(f32, 8 * inner, rows),
            group_stat=vm(f32, 8 * outer, rows),
            stat_sems=dma((2,)),
            group_sems=dma((2,)),
            got_sems=dma((2,)),
            level_sems=dma((2,)),
            final_sems=dma((2,)),
        )

    regular = pltpu.SemaphoreType.REGULAR((max(seq_count - 2, 1),))
    scratch = dict(
        q_buf=vm(bf16, *queries.shape),
        fresh_buf=vm(bf16, *fresh.shape),
        res_buf=vm(bf16, 2, resident, res_rows, head_dim),
        table=pltpu.SMEM(block_table.shape, i32),
        lengths=pltpu.SMEM(lengths.shape, i32),
        joins=pltpu.SMEM((1, 1), i32),
        slot_of=pltpu.SMEM((senders,), i32),
        sources=pltpu.SMEM((slot_count,), i32),
        arrived=vm(bf16, seq_count, head_count, 2, block_len, head_dim),
        turned=vm(f32, rows, rows),
        own_sem=dma,
        table_sem=dma,
        q_sem=dma,
        fresh_sem=dma,
        lengths_sem=dma,
        joins_sem=dma,
        res_sems=dma((resident, chunks)),
        block_send=dma,
        block_recv=dma,
        held_send=dma,
        held_recv=dma((head_count,)),
        above_sems=regular,
        below_sems=regular,
        held=[vm(bf16, 2, dev_blocks, block_len, head_dim) for _ in range(head_count)],
        staged=[vm(bf16, seq_count, 2, block_len, head_dim) for _ in range(head_count)],
        batch_a=batch(resident, part),
        batch_b=batch(1, rows),
    )
    inputs = dict(
        q_hbm=queries,
        fresh_hbm=fresh,
        prefill_hbm=prefill,
        table_hbm=block_table,
        lengths_hbm=lengths,
        joins_hbm=join_step.reshape(1, 1),
        res_hbm=res_kv.reshape(2, resident, res_rows, head_dim),
    )
    outputs = dict(
        attn_out=pltpu.VMEM(queries.shape, bf16),
        cache_out=pltpu.VMEM((2, 1, slot_count * block_len, head_dim), bf16),
    )
    operands = jax.tree.leaves(inputs)
    tree = jax.tree.structure((inputs, outputs, scratch))
    out_bytes = 2 * (queries.size + 2 * slot_count * block_len * head_dim)
    attn, cache = pl.pallas_call(
        functools.partial(kernel, seq_count, head_count, tree),
        out_shape=tuple(jax.tree.leaves(outputs)),
        in_specs=[hbm] * len(operands),
        out_specs=(vmem, vmem),
        scratch_shapes=jax.tree.leaves(scratch),
        compiler_params=pltpu.CompilerParams(
            collective_id=0, has_side_effects=True, vmem_limit_bytes=62 * 2**20 - 3 * out_bytes
        ),
    )(*operands)
    return pl.pallas_call(
        store_kernel,
        out_shape=(
            jax.ShapeDtypeStruct(attn.shape, bf16),
            jax.ShapeDtypeStruct(cache.shape, bf16),
        ),
        in_specs=[vmem, vmem],
        out_specs=(hbm, hbm),
        scratch_shapes=[dma((3,))],
        compiler_params=pltpu.CompilerParams(vmem_limit_bytes=2**20),
    )(pltpu.with_memory_space_constraint(attn, pltpu.VMEM), pltpu.with_memory_space_constraint(cache, pltpu.VMEM))


def solution(mesh):
    in_specs = (
        P("groups", None, "head", None),
        P("groups", None, None, "head", None),
        P("groups", None, "seq", "head", None),
        P("groups", None, ("seq", "head"), None),
        P("groups"),
        P("groups"),
        P("groups"),
    )
    out_specs = (P("groups", None, "head", None), P("groups", "head", "seq", None))
    body = functools.partial(per_device, mesh.shape["seq"], mesh.shape["head"])
    return jax.shard_map(body, mesh=mesh, in_specs=in_specs, out_specs=out_specs, check_vma=False)
```

time: 30.5 us -> 24.3 us (0.80)
  Pallas kernels: 27.7 us -> 22.8 us
  local copies, waits for them, and re-layouts: 1.44 us -> 0 us
    pallas_call x1 -> x2, Pallas kernels: 27.7 us -> 22.8 us  [the longest x1 22 us: per_device(): pl.pallas_call(functools.partial(kernel, seq_count, head_count, tree), ou...]
    unnamed x2 -> x0, local copies, waits for them, and re-layouts: 1.44 us -> none
where the time goes in v1:
time: 24.3 us; the launch traced here: 24.1 us
  Pallas kernels  22.8 us (94%)
  between operations  1.29 us (5%)
    pallas_call x1, Pallas kernels, per_device(): pl.pallas_call(functools.partial(kernel, seq_count, head_count, tree), ou...  22 us
    pallas_call x1, Pallas kernels, per_device(): pl.pallas_call(store_kernel, out_shape=(jax.ShapeDtypeStruct(attn.shape,...  0.84 us

profile of v1, /device:TPU:0, one launch (start us, length us, event | category | flops | bytes accessed | tf_op | source)
XLA Modules:
  0.0 24.1 jit_solution(11127551751919156750)
XLA Ops:
  1.3 22.0 %shard_map.86 = (bf16[16,3,8,128]{3,2,1,0:T(8,128)(2,1)S(1)}, bf16[2,1,1024,128]{3,2,1,0:T(8,128)(2,1)S(1)}) custom-call(bf16[2,3,16,128]{3,2,1,0:T(8,128)(2,1)} %bitcast.9, s32[1,1]{1,0:T(1,128)} %bitcast.6.leaves_1_, s32[3]{0:T(128)} %leaves_2_.1, bf16[2,4,4,64,128]{4,3,2,1,0:T(8,128)(2,1)} %bitcast.8, bf16[16,3,8,128]{3,2,1,0:T(8,128)(2,1)} %leaves_4_.1, ...), custom_call_target="tpu_custom_call" | custom-call | tf_op jit(solution)/shard_map/pallas_call | solution.py:514
  23.3 0.8 %shard_map.87 = (bf16[16,3,8,128]{3,2,1,0:T(8,128)(2,1)}, bf16[2,1,1024,128]{3,2,1,0:T(8,128)(2,1)}) custom-call(bf16[16,3,8,128]{3,2,1,0:T(8,128)(2,1)S(1)} %get-tuple-element.4.attn, bf16[2,1,1024,128]{3,2,1,0:T(8,128)(2,1)S(1)} %get-tuple-element.5.cache), custom_call_target="tpu_custom_call" | custom-call | tf_op jit(solution)/shard_map/pallas_call | solution.py:524

commit v2 on v1

--- a/solution.py
+++ b/solution.py
@@ -96,6 +96,7 @@
 
     table_copy = local(ref.table_hbm, table, ref.table_sem)
     own_copy = local(prefill_hbm.at[:, head_index], held[0], ref.own_sem)
+    all_copy = local(prefill_hbm, ref.all_buf, ref.all_sem)
     q_copy = local(q_hbm, ref.q_buf, ref.q_sem)
     fresh_copy = local(fresh_hbm, ref.fresh_buf, ref.fresh_sem)
     length_copy = local(ref.lengths_hbm, lengths, ref.lengths_sem)
@@ -154,13 +155,14 @@
                     remote(staged[o].at[peer], target, ref.block_send, ref.block_recv, seq=peer)
 
     def hand(o):
-        remote(prefill_hbm.at[:, heads[o]], held[o], ref.held_send, ref.held_recv.at[o], head=heads[o])
+        remote(ref.all_buf.at[:, heads[o]], held[o], ref.held_send, ref.held_recv.at[o], head=heads[o])
 
     far_first = range(seq_count - 1, 0, -1)
     stage(0)
+    all_copy.wait()
     pl.semaphore_wait(barrier, head_count - 1 + above.astype(jnp.int32) + below.astype(jnp.int32))
     tell(1)
-    for o in range(1, min(3, head_count)):
+    for o in range(1, head_count):
         hand(o)
     forward(0, [1])
 
@@ -244,7 +246,7 @@
 
         def share(self, target, back, sems, peer):
             source = self.refs.stat_send.at[0 if target is self.refs.stat else 1]
-            remote(source, target.at[pl.ds(8 * back, 8)], sems.at[0], sems.at[1], seq=peer)
+            remote(source.at[pl.ds(0, 2 * self.count)], target.at[pl.ds(8 * back, 2 * self.count)], sems.at[0], sems.at[1], seq=peer)
 
         def columns(self, tiles, members):
             stats = tiles[0 : 8 * members]
@@ -262,7 +264,7 @@
         def across(self):
             refs = self.refs
             if inner > 1:
-                drain(refs.stat.at[pl.ds(8, 8 * (inner - 1))], refs.stat_sems.at[1])
+                drain(refs.stat.at[pl.ds(0, 2 * self.count * (inner - 1))], refs.stat_sems.at[1])
             turned = self.columns(refs.stat, inner)
             if self.split:
                 ref.turned[...] = turned
@@ -286,7 +288,7 @@
 
         def finish(self):
             refs, level = self.refs, self.refs.level
-            drain(refs.group_stat.at[pl.ds(8, 8 * (outer - 1))], refs.group_sems.at[1])
+            drain(refs.group_stat.at[pl.ds(0, 2 * self.count * (outer - 1))], refs.group_sems.at[1])
             turned = self.columns(refs.group_stat, outer)[0 : self.size]
             drain(level.at[pl.ds(1, outer - 1)], refs.level_sems.at[1])
             offset = place_in * step_part if self.split else 0
@@ -316,8 +318,8 @@
                 drain(others, refs.final_sems.at[0])
             if inner > 1:
                 drain(refs.got.at[pl.ds(1, inner - 1)], refs.got_sems.at[0])
-                drain(refs.stat.at[pl.ds(8, 8 * (inner - 1))], refs.stat_sems.at[0])
-            drain(refs.group_stat.at[pl.ds(8, 8 * (outer - 1))], refs.group_sems.at[0])
+                drain(refs.stat.at[pl.ds(0, 2 * self.count * (inner - 1))], refs.stat_sems.at[0])
+            drain(refs.group_stat.at[pl.ds(0, 2 * self.count * (outer - 1))], refs.group_sems.at[0])
             drain(refs.level.at[pl.ds(1, outer - 1)], refs.level_sems.at[0])
 
     def take(o):
@@ -330,8 +332,6 @@
             forward(0, [2])
 
     results = [attend_resident(0, between)]
-    for o in range(3, head_count):
-        hand(o)
     for d in range(3, seq_count):
         learn(d)
         forward(0, [d])
@@ -478,6 +478,8 @@
         arrived=vm(bf16, seq_count, head_count, 2, block_len, head_dim),
         turned=vm(f32, rows, rows),
         own_sem=dma,
+        all_sem=dma,
+        all_buf=vm(bf16, *prefill.shape),
         table_sem=dma,
         q_sem=dma,
         fresh_sem=dma,

time: 24.3 us -> 24 us (0.988)
    pallas_call x1, Pallas kernels: 22 us -> 21.7 us  [per_device(): pl.pallas_call(functools.partial(kernel, seq_count, head_count, tree), ou...]
where the time goes in v2:
time: 24 us; the launch traced here: 23.8 us
  Pallas kernels  22.6 us (94%)
  between operations  1.29 us (5%)
    pallas_call x1, Pallas kernels, per_device(): pl.pallas_call(functools.partial(kernel, seq_count, head_count, tree), ou...  21.7 us
    pallas_call x1, Pallas kernels, per_device(): pl.pallas_call(store_kernel, out_shape=(jax.ShapeDtypeStruct(attn.shape,...  0.84 us

profile of v2, /device:TPU:0, one launch (start us, length us, event | category | flops | bytes accessed | tf_op | source)
XLA Modules:
  0.0 23.8 jit_solution(5190642653584255384)
XLA Ops:
  1.3 21.7 %shard_map.86 = (bf16[16,3,8,128]{3,2,1,0:T(8,128)(2,1)S(1)}, bf16[2,1,1024,128]{3,2,1,0:T(8,128)(2,1)S(1)}) custom-call(bf16[2,3,16,128]{3,2,1,0:T(8,128)(2,1)} %bitcast.9, s32[1,1]{1,0:T(1,128)} %bitcast.6.leaves_1_, s32[3]{0:T(128)} %leaves_2_.1, bf16[2,4,4,64,128]{4,3,2,1,0:T(8,128)(2,1)} %bitcast.8, bf16[16,3,8,128]{3,2,1,0:T(8,128)(2,1)} %leaves_4_.1, ...), custom_call_target="tpu_custom_call" | custom-call | tf_op jit(solution)/shard_map/pallas_call | solution.py:516
  23.0 0.8 %shard_map.87 = (bf16[16,3,8,128]{3,2,1,0:T(8,128)(2,1)}, bf16[2,1,1024,128]{3,2,1,0:T(8,128)(2,1)}) custom-call(bf16[16,3,8,128]{3,2,1,0:T(8,128)(2,1)S(1)} %get-tuple-element.4.attn, bf16[2,1,1024,128]{3,2,1,0:T(8,128)(2,1)S(1)} %get-tuple-element.5.cache), custom_call_target="tpu_custom_call" | custom-call | tf_op jit(solution)/shard_map/pallas_call | solution.py:526

commit v3 on v2

--- a/solution.py
+++ b/solution.py
@@ -165,6 +165,9 @@
     for o in range(1, head_count):
         hand(o)
     forward(0, [1])
+    if seq_count > 2:
+        learn(2)
+        forward(0, [2])
 
     def query_rows(r):
         wide = ref.q_buf[:, r].astype(jnp.float32).reshape(rows, head_dim)
@@ -327,14 +330,12 @@
         stage(o)
 
     def between(k):
-        if k == 0 and seq_count > 2:
-            learn(2)
-            forward(0, [2])
+        if k == 0:
+            for d in range(3, seq_count):
+                learn(d)
+                forward(0, [d])
 
     results = [attend_resident(0, between)]
-    for d in range(3, seq_count):
-        learn(d)
-        forward(0, [d])
     take(1)
     forward(1, far_first, False)
     results += [attend_resident(r) for r in range(1, resident)]

time: 24 us -> 23.7 us (0.987)
  Pallas kernels: 22.6 us -> 22.2 us
    pallas_call x1, Pallas kernels: 21.7 us -> 21.4 us  [per_device(): pl.pallas_call(functools.partial(kernel, seq_count, head_count, tree), ou...]
where the time goes in v3:
time: 23.7 us; the launch traced here: 23.5 us
  Pallas kernels  22.2 us (94%)
  between operations  1.29 us (5%)
    pallas_call x1, Pallas kernels, per_device(): pl.pallas_call(functools.partial(kernel, seq_count, head_count, tree), ou...  21.4 us
    pallas_call x1, Pallas kernels, per_device(): pl.pallas_call(store_kernel, out_shape=(jax.ShapeDtypeStruct(attn.shape,...  0.84 us

profile of v3, /device:TPU:0, one launch (start us, length us, event | category | flops | bytes accessed | tf_op | source)
XLA Modules:
  0.0 23.5 jit_solution(9621856913214585927)
XLA Ops:
  1.3 21.4 %shard_map.86 = (bf16[16,3,8,128]{3,2,1,0:T(8,128)(2,1)S(1)}, bf16[2,1,1024,128]{3,2,1,0:T(8,128)(2,1)S(1)}) custom-call(bf16[2,3,16,128]{3,2,1,0:T(8,128)(2,1)} %bitcast.9, s32[1,1]{1,0:T(1,128)} %bitcast.6.leaves_1_, s32[3]{0:T(128)} %leaves_2_.1, bf16[2,4,4,64,128]{4,3,2,1,0:T(8,128)(2,1)} %bitcast.8, bf16[16,3,8,128]{3,2,1,0:T(8,128)(2,1)} %leaves_4_.1, ...), custom_call_target="tpu_custom_call" | custom-call | tf_op jit(solution)/shard_map/pallas_call | solution.py:517
  22.7 0.8 %shard_map.87 = (bf16[16,3,8,128]{3,2,1,0:T(8,128)(2,1)}, bf16[2,1,1024,128]{3,2,1,0:T(8,128)(2,1)}) custom-call(bf16[16,3,8,128]{3,2,1,0:T(8,128)(2,1)S(1)} %get-tuple-element.4.attn, bf16[2,1,1024,128]{3,2,1,0:T(8,128)(2,1)S(1)} %get-tuple-element.5.cache), custom_call_target="tpu_custom_call" | custom-call | tf_op jit(solution)/shard_map/pallas_call | solution.py:527
